TPU v7x, 128 devices: a whole 4x4x4 slice. The times are simulated.
128 devices in a mesh: py: 4 (over y), px: 8 (over z_lo, x), pz: 4 (over z_hi, core).
Axes of the slice: x: 4, y: 4, z: 4 (z_hi: 2, z_lo: 2; z = z_hi * 2 + z_lo), core: 2. Of those that a mesh axis runs over, the one named last changes fastest.
Arguments:
- starting_state: float32 [512, 32, 128, 128], P('py', 'px', 'pz'), may hold values from 0.5 to 2
- scaled_conductivity: float32 [512, 32, 128, 128], P('py', 'px', 'pz'), may hold values from 0.03 to 0.15
- scaled_heat_supply: float32 [512, 32, 128, 128], P('py', 'px', 'pz'), may hold values from -0.2 to 0.2
Outputs:
- normalised_result: float32 [512, 32, 128, 128], P('py', 'px', 'pz')
- temperature_end: float32 [512, 32, 128, 128], P('py', 'px', 'pz')
All inputs are finite; a program needn't handle non-finite values.
Results may differ from a plain program's by a relative error of at most 0.00002.
Values sent between devices are 32-bit elements; how exact they have to be, the bound alone decides.
A program may use at most 128 MiB of HBM per device.

v0:
```python
import jax
import jax.numpy as jnp
from jax import lax
from jax.sharding import PartitionSpec as P

STEPS = 4


def extended(array, sides, width):
    edges = {}
    for axis, dim in sides:
        devices, length = (lax.axis_size(axis), array.shape[dim])
        up = [(i, (i + 1) % devices) for i in range(devices - 1)]
        last = lax.slice_in_dim(array, length - width, length, axis=dim)
        initial = lax.slice_in_dim(array, 0, width, axis=dim)
        edges[dim] = (
            lax.ppermute(last, axis, up),
            lax.ppermute(initial, axis, [(b, a) for a, b in up]),
        )
    done = []
    for _, dim in sides:
        low, high = edges[dim]
        around = [(width, width) if d in done else (0, 0) for d in range(array.ndim)]
        array = jnp.concatenate([jnp.pad(low, around), array, jnp.pad(high, around)], axis=dim)
        done.append(dim)
    return array


def interior_points(values, dims):
    for coordinate_axis in dims:
        values = lax.slice_in_dim(
            values, 1, values.shape[coordinate_axis] - 1, axis=coordinate_axis
        )
    return values


def boundary_layer(values, coordinate_axis, start, dims):
    others = [other for other in dims if other != coordinate_axis]
    values = interior_points(values, others)
    return lax.slice_in_dim(
        values, start, start + values.shape[coordinate_axis] - 2, axis=coordinate_axis
    )


def conduction_timestep(framed_thermal_lattice, scaled_conductivity, scaled_heat_supply):
    central_point = interior_points(framed_thermal_lattice, (0, 1, 2))
    preceding_neighbour = [
        boundary_layer(framed_thermal_lattice, coordinate_axis, 0, (0, 1, 2))
        for coordinate_axis in (0, 1, 2)
    ]
    following_neighbour = [
        boundary_layer(framed_thermal_lattice, coordinate_axis, 2, (0, 1, 2))
        for coordinate_axis in (0, 1, 2)
    ]
    spread = (
        preceding_neighbour[0]
        + following_neighbour[0]
        + preceding_neighbour[1]
        + following_neighbour[1]
        + preceding_neighbour[2]
        + following_neighbour[2]
        - 6.0 * central_point
    )
    return central_point + scaled_conductivity * spread + scaled_heat_supply


def body(starting_state, scaled_conductivity, scaled_heat_supply):
    for step in range(STEPS):
        framed_thermal_lattice = extended(starting_state, (("py", 0), ("px", 1), ("pz", 2)), 1)
        starting_state = conduction_timestep(
            framed_thermal_lattice, scaled_conductivity, scaled_heat_supply
        )
    row_number_total = starting_state.shape[1] * lax.axis_size("px")
    guess = 1.0
    moved = starting_state - guess
    totals, squares = lax.psum(
        (jnp.sum(moved, axis=1, keepdims=True), jnp.sum(moved * moved, axis=1, keepdims=True)), "px"
    )
    row_average = guess + totals / row_number_total
    deviation_rows = starting_state - row_average
    line_variance = squares / row_number_total - totals / row_number_total * (
        totals / row_number_total
    )
    normalised_result = deviation_rows * lax.rsqrt(line_variance + 0.0001)
    return (normalised_result, starting_state)


def solution(mesh):
    placed = (P("py", "px", "pz", None), P("py", "px", "pz", None), P("py", "px", "pz", None))
    return jax.shard_map(
        body,
        mesh=mesh,
        in_specs=placed,
        out_specs=(P("py", "px", "pz", None), P("py", "px", "pz", None)),
        check_vma=False,
    )
```

profile of v0, /device:TPU:1, one launch (start us, length us, event | category | flops | bytes accessed | tf_op | source)
XLA Modules:
  0.0 497.5 jit_solution(4713084273634273184)
XLA Ops:
  7.2 8.2 %copy.16 = f32[128,4,32,128]{3,0,2,1:T(8,128)S(1)} copy(f32[128,4,32,128]{3,2,1,0:T(8,128)} %param.3) | data formatting | bytes 16777216 | tf_op args[0]
  16.0 4.1 collective-permute-start.2
  21.4 6.3 %collective-permute-start.4 = (f32[128,4,1,128]{3,0,2,1:T(8,128)S(1)}, f32[128,4,1,128]{3,0,2,1:T(8,128)S(1)}, u32[]{:S(2)}, u32[]{:S(2)}) collective-permute-start(f32[128,4,1,128]{3,0,2,1:T(8,128)S(1)} %get-tuple-element.27), channel_id=1, source_target_pairs={{0,1},{1,2},{2,3},{4,5},{5,6},{6,7},{8,9},{9,10},{10,11},{12,13},{... | collective-permute-start | bytes 786440 | tf_op jit(solution)/shard_map/ppermute | solution.py:17
  27.7 1.9 collective-permute-start.5
  30.5 1.3 collective-permute-start.1
  31.8 32.3 %collective-permute-done.2 = f32[128,1,32,128]{3,0,2,1:T(8,128)S(1)} collective-permute-done((f32[128,1,32,128]{3,0,2,1:T(8,128)S(1)}, f32[128,1,32,128]{3,0,2,1:T(8,128)S(1)}, u32[]{:S(2)}, u32[]{:S(2)}) %collective-permute-start.2) | collective-permute-done | bytes 2097184 | tf_op jit(solution)/shard_map/ppermute | solution.py:17
  64.2 3.4 collective-permute-start
  68.7 2.0 collective-permute-done.4
  70.7 3.7 collective-permute-done.5
  74.4 29.5 %fusion.38 = f32[128,4,32,128]{3,0,2,1:T(8,128)} fusion(f32[128,4,32,128]{3,0,2,1:T(8,128)} %copy-done, f32[128,4,1,128]{3,0,2,1:T(8,128)S(1)} %collective-permute-done.5, f32[130,1,32,128]{3,0,2,1:T(8,128)S(1)} %pad.51, f32[130,1,32,128]{3,0,2,1:T(8,128)S(1)} %pad.50, f32[1,4,32,128]{3,0,2,1:T(1,128)S(1)} %collective-permute-done.1, ...), kind=kLoop, calls=%fused_computation.93 | loop fusion | flops 71303168 | bytes 38469632 | tf_op jit(solution)/shard_map/add | solution.py:64
  104.0 2.5 fusion.53
  106.5 1.4 collective-permute-start.8
  110.3 5.2 %collective-permute-start.10 = (f32[128,4,1,128]{3,0,2,1:T(8,128)S(1)}, f32[128,4,1,128]{3,0,2,1:T(8,128)S(1)}, u32[]{:S(2)}, u32[]{:S(2)}) collective-permute-start(f32[128,4,1,128]{3,0,2,1:T(8,128)S(1)} %get-tuple-element.21), channel_id=1, source_target_pairs={{0,1},{1,2},{2,3},{4,5},{5,6},{6,7},{8,9},{9,10},{10,11},{12,13},{... | collective-permute-start | bytes 786440 | tf_op jit(solution)/shard_map/ppermute | solution.py:17
  115.4 1.9 collective-permute-start.11
  117.4 1.3 fusion.52
  118.7 4.0 collective-permute-start.6
  122.7 30.5 %collective-permute-done.8 = f32[128,1,32,128]{3,0,2,1:T(8,128)S(1)} collective-permute-done((f32[128,1,32,128]{3,0,2,1:T(8,128)S(1)}, f32[128,1,32,128]{3,0,2,1:T(8,128)S(1)}, u32[]{:S(2)}, u32[]{:S(2)}) %collective-permute-start.8) | collective-permute-done | bytes 2097184 | tf_op jit(solution)/shard_map/ppermute | solution.py:17
  154.7 2.5 collective-permute-done.9
  158.2 3.4 collective-permute-done.11
  161.5 29.5 %fusion.27 = f32[128,4,32,128]{3,0,2,1:T(8,128)} fusion(f32[128,4,32,128]{3,0,2,1:T(8,128)} %fusion.38, f32[128,4,1,128]{3,0,2,1:T(8,128)S(1)} %collective-permute-done.11, f32[130,1,32,128]{3,0,2,1:T(8,128)S(1)} %pad.55, f32[130,1,32,128]{3,0,2,1:T(8,128)S(1)} %pad.54, f32[1,4,32,128]{3,0,2,1:T(1,128)S(1)} %collective-permute-done.7, ...), kind=kLoop, calls=%fused_computation.64 | loop fusion | flops 71303168 | bytes 38469632 | tf_op jit(solution)/shard_map/add | solution.py:64
  191.1 2.5 fusion.50
  193.6 1.8 collective-permute-start.14
  195.4 1.3 collective-permute-start.15
  197.8 3.9 collective-permute-start.16
  201.6 1.9 collective-permute-start.17
  203.6 1.3 fusion.49
  204.9 3.6 collective-permute-start.12
  208.5 30.4 %collective-permute-done.14 = f32[128,1,32,128]{3,0,2,1:T(8,128)S(1)} collective-permute-done((f32[128,1,32,128]{3,0,2,1:T(8,128)S(1)}, f32[128,1,32,128]{3,0,2,1:T(8,128)S(1)}, u32[]{:S(2)}, u32[]{:S(2)}) %collective-permute-start.14) | collective-permute-done | bytes 2097184 | tf_op jit(solution)/shard_map/ppermute | solution.py:17
  240.4 2.9 collective-permute-done.15
  243.5 1.5 collective-permute-done.13
  244.9 2.5 collective-permute-done.17
  247.4 29.5 %fusion.16 = f32[128,4,32,128]{3,0,2,1:T(8,128)} fusion(f32[128,4,32,128]{3,0,2,1:T(8,128)} %fusion.27, f32[128,4,1,128]{3,0,2,1:T(8,128)S(1)} %collective-permute-done.17, f32[130,1,32,128]{3,0,2,1:T(8,128)S(1)} %pad.59, f32[130,1,32,128]{3,0,2,1:T(8,128)S(1)} %pad.58, f32[1,4,32,128]{3,0,2,1:T(1,128)S(1)} %collective-permute-done.13, ...), kind=kLoop, calls=%fused_computation.35 | loop fusion | flops 71303168 | bytes 38469632 | tf_op jit(solution)/shard_map/add | solution.py:64
  276.9 2.5 fusion.46
  279.4 1.5 collective-permute-start.20
  283.3 2.1 collective-permute-start.22
  285.4 3.6 collective-permute-start.23
  289.1 1.3 fusion.47
  290.4 3.6 collective-permute-start.18
  294.0 29.5 %collective-permute-done.20 = f32[128,1,32,128]{3,0,2,1:T(8,128)S(1)} collective-permute-done((f32[128,1,32,128]{3,0,2,1:T(8,128)S(1)}, f32[128,1,32,128]{3,0,2,1:T(8,128)S(1)}, u32[]{:S(2)}, u32[]{:S(2)}) %collective-permute-start.20) | collective-permute-done | bytes 2097184 | tf_op jit(solution)/shard_map/ppermute | solution.py:17
  325.0 2.5 collective-permute-done.21
  327.5 1.5 pad.63
  329.0 2.3 collective-permute-done.23
  331.3 32.9 %add_reduce_fusion = (f32[128,32,128]{2,0,1:T(8,128)}, f32[128,32,128]{2,0,1:T(8,128)}, f32[128,4,32,128]{3,0,2,1:T(8,128)}) fusion(f32[128,4,32,128]{3,2,1,0:T(8,128)} %param.5, f32[128,4,32,128]{3,0,2,1:T(8,128)} %fusion.16, f32[128,4,1,128]{3,0,2,1:T(8,128)S(1)} %collective-permute-done.23, f32[130,1,32,128]{3,0,2,1:T(8,128)} %pad.63, ...), kind=kLoop, calls=%fused_computation.120 | loop fusion | flops 78643200 | bytes 42663936 | tf_op jit(solution)/shard_map/reduce_sum | solution.py:77
  364.2 11.6 %copy.25 = f32[128,4,32,128]{3,2,1,0:T(8,128)} copy(f32[128,4,32,128]{3,0,2,1:T(8,128)} %get-tuple-element.8) | data formatting | bytes 16777216
  375.9 95.2 %all-reduce.19.cloned.1.call-done = (f32[128,1,32,128]{3,0,2,1:T(8,128)}, f32[128,1,32,128]{3,0,2,1:T(8,128)}) async-done(((f32[128,1,32,128]{3,0,2,1:T(8,128)}, f32[128,1,32,128]{3,0,2,1:T(8,128)}), (f32[128,1,32,128]{3,0,2,1:T(8,128)}, f32[128,1,32,128]{3,0,2,1:T(8,128)})) %all-reduce.19.cloned.1.call-update) | async-done | bytes 4194320 | tf_op jit(solution)/shard_map/psum | solution.py:76
  471.0 5.1 %add_bitcast_fusion = (f32[128,32,128]{2,0,1:T(8,128)}, f32[128,32,128]{2,0,1:T(8,128)}) fusion(f32[128,1,32,128]{3,0,2,1:T(8,128)} %get-tuple-element.7, f32[128,1,32,128]{3,0,2,1:T(8,128)} %get-tuple-element.6), kind=kLoop, calls=%fused_computation.122 | loop fusion | flops 3145728 | bytes 8388608 | tf_op jit(solution)/shard_map/sub | solution.py:80
  476.1 6.1 %subtract_multiply_fusion = f32[128,4,32,128]{3,0,2,1:T(8,128)S(1)} fusion(f32[128,4,32,128]{3,0,2,1:T(8,128)} %get-tuple-element.8, f32[128,32,128]{2,0,1:T(8,128)} %get-tuple-element.34, f32[128,32,128]{2,0,1:T(8,128)} %get-tuple-element.33), kind=kLoop, calls=%fused_computation.119 | loop fusion | flops 4194304 | bytes 20971520 | tf_op jit(solution)/shard_map/mul | solution.py:84
  482.2 8.3 %copy.24 = f32[128,4,32,128]{3,2,1,0:T(8,128)} copy(f32[128,4,32,128]{3,0,2,1:T(8,128)S(1)} %subtract_multiply_fusion) | data formatting | bytes 16777216
  (34 shorter events, 15.2 us)
Async XLA Ops:
  7.2 463.9 %all-reduce.19.cloned.1.call-start = ((), (), s32[]{:S(2)}) async-start(), calls=%async_computation | async-start | bytes 8388608 | tf_op jit(solution)/shard_map/psum | solution.py:76
  15.4 52.9 %copy-start = (f32[128,4,32,128]{3,0,2,1:T(8,128)}, f32[128,4,32,128]{3,0,2,1:T(8,128)S(1)}, u32[]{:S(2)}) copy-start(f32[128,4,32,128]{3,0,2,1:T(8,128)S(1)} %copy.16) | copy-start | bytes 25165828
  16.0 48.2 %collective-permute-start.2 = (f32[128,1,32,128]{3,0,2,1:T(8,128)S(1)}, f32[128,1,32,128]{3,0,2,1:T(8,128)S(1)}, u32[]{:S(2)}, u32[]{:S(2)}) collective-permute-start(f32[128,1,32,128]{3,0,2,1:T(8,128)S(1)} %get-tuple-element.31), channel_id=1, source_target_pairs={{0,4},{4,8},{8,12},{12,16},{16,20},{20,24},{24,28},{1,5},{5,9},{9,... | collective-permute-start | bytes 6291464 | tf_op jit(solution)/shard_map/ppermute | solution.py:17
  20.0 48.1 %collective-permute-start.3 = (f32[128,1,32,128]{3,0,2,1:T(8,128)S(1)}, f32[128,1,32,128]{3,0,2,1:T(8,128)S(1)}, u32[]{:S(2)}, u32[]{:S(2)}) collective-permute-start(f32[128,1,32,128]{3,0,2,1:T(8,128)S(1)} %get-tuple-element.32), channel_id=1, source_target_pairs={{4,0},{8,4},{12,8},{16,12},{20,16},{24,20},{28,24},{5,1},{9,5},{13... | collective-permute-start | bytes 6291464 | tf_op jit(solution)/shard_map/ppermute | solution.py:18
  21.4 49.3 %collective-permute-start.4 = (f32[128,4,1,128]{3,0,2,1:T(8,128)S(1)}, f32[128,4,1,128]{3,0,2,1:T(8,128)S(1)}, u32[]{:S(2)}, u32[]{:S(2)}) collective-permute-start(f32[128,4,1,128]{3,0,2,1:T(8,128)S(1)} %get-tuple-element.27), channel_id=1, source_target_pairs={{0,1},{1,2},{2,3},{4,5},{5,6},{6,7},{8,9},{9,10},{10,11},{12,13},{... | collective-permute-start | bytes 786440 | tf_op jit(solution)/shard_map/ppermute | solution.py:17
  27.7 46.7 %collective-permute-start.5 = (f32[128,4,1,128]{3,0,2,1:T(8,128)S(1)}, f32[128,4,1,128]{3,0,2,1:T(8,128)S(1)}, u32[]{:S(2)}, u32[]{:S(2)}) collective-permute-start(f32[128,4,1,128]{3,0,2,1:T(8,128)S(1)} %get-tuple-element.28), channel_id=1, source_target_pairs={{1,0},{2,1},{3,2},{5,4},{6,5},{7,6},{9,8},{10,9},{11,10},{13,12},{... | collective-permute-start | bytes 786440 | tf_op jit(solution)/shard_map/ppermute | solution.py:18
  30.5 37.8 %collective-permute-start.1 = (f32[1,4,32,128]{3,0,2,1:T(1,128)S(1)}, f32[1,4,32,128]{3,0,2,1:T(1,128)S(1)}, u32[]{:S(2)}, u32[]{:S(2)}) collective-permute-start(f32[1,4,32,128]{3,0,2,1:T(1,128)S(1)} %bitcast.11), channel_id=1, source_target_pairs={{32,0},{64,32},{96,64},{33,1},{65,33},{97,65},{34,2},{66,34},{98,6... | collective-permute-start | bytes 196616 | tf_op jit(solution)/shard_map/ppermute | solution.py:18
  64.2 4.5 collective-permute-start
  106.5 46.7 %collective-permute-start.8 = (f32[128,1,32,128]{3,0,2,1:T(8,128)S(1)}, f32[128,1,32,128]{3,0,2,1:T(8,128)S(1)}, u32[]{:S(2)}, u32[]{:S(2)}) collective-permute-start(f32[128,1,32,128]{3,0,2,1:T(8,128)S(1)} %get-tuple-element.25), channel_id=1, source_target_pairs={{0,4},{4,8},{8,12},{12,16},{16,20},{20,24},{24,28},{1,5},{5,9},{9,... | collective-permute-start | bytes 6291464 | tf_op jit(solution)/shard_map/ppermute | solution.py:17
  107.9 49.3 %collective-permute-start.9 = (f32[128,1,32,128]{3,0,2,1:T(8,128)S(1)}, f32[128,1,32,128]{3,0,2,1:T(8,128)S(1)}, u32[]{:S(2)}, u32[]{:S(2)}) collective-permute-start(f32[128,1,32,128]{3,0,2,1:T(8,128)S(1)} %get-tuple-element.26), channel_id=1, source_target_pairs={{4,0},{8,4},{12,8},{16,12},{20,16},{24,20},{28,24},{5,1},{9,5},{13... | collective-permute-start | bytes 6291464 | tf_op jit(solution)/shard_map/ppermute | solution.py:18
  110.3 47.9 %collective-permute-start.10 = (f32[128,4,1,128]{3,0,2,1:T(8,128)S(1)}, f32[128,4,1,128]{3,0,2,1:T(8,128)S(1)}, u32[]{:S(2)}, u32[]{:S(2)}) collective-permute-start(f32[128,4,1,128]{3,0,2,1:T(8,128)S(1)} %get-tuple-element.21), channel_id=1, source_target_pairs={{0,1},{1,2},{2,3},{4,5},{5,6},{6,7},{8,9},{9,10},{10,11},{12,13},{... | collective-permute-start | bytes 786440 | tf_op jit(solution)/shard_map/ppermute | solution.py:17
  115.4 46.1 %collective-permute-start.11 = (f32[128,4,1,128]{3,0,2,1:T(8,128)S(1)}, f32[128,4,1,128]{3,0,2,1:T(8,128)S(1)}, u32[]{:S(2)}, u32[]{:S(2)}) collective-permute-start(f32[128,4,1,128]{3,0,2,1:T(8,128)S(1)} %get-tuple-element.22), channel_id=1, source_target_pairs={{1,0},{2,1},{3,2},{5,4},{6,5},{7,6},{9,8},{10,9},{11,10},{13,12},{... | collective-permute-start | bytes 786440 | tf_op jit(solution)/shard_map/ppermute | solution.py:18
  118.7 38.7 %collective-permute-start.6 = (f32[1,4,32,128]{3,0,2,1:T(1,128)S(1)}, f32[1,4,32,128]{3,0,2,1:T(1,128)S(1)}, u32[]{:S(2)}, u32[]{:S(2)}) collective-permute-start(f32[1,4,32,128]{3,0,2,1:T(1,128)S(1)} %get-tuple-element.23), channel_id=1, source_target_pairs={{0,32},{32,64},{64,96},{1,33},{33,65},{65,97},{2,34},{34,66},{66,9... | collective-permute-start | bytes 196616 | tf_op jit(solution)/shard_map/ppermute | solution.py:17
  153.2 5.0 %collective-permute-start.7 = (f32[1,4,32,128]{3,0,2,1:T(1,128)S(1)}, f32[1,4,32,128]{3,0,2,1:T(1,128)S(1)}, u32[]{:S(2)}, u32[]{:S(2)}) collective-permute-start(f32[1,4,32,128]{3,0,2,1:T(1,128)S(1)} %get-tuple-element.24), channel_id=1, source_target_pairs={{32,0},{64,32},{96,64},{33,1},{65,33},{97,65},{34,2},{66,34},{98,6... | collective-permute-start | bytes 196616 | tf_op jit(solution)/shard_map/ppermute | solution.py:18
  193.6 45.3 %collective-permute-start.14 = (f32[128,1,32,128]{3,0,2,1:T(8,128)S(1)}, f32[128,1,32,128]{3,0,2,1:T(8,128)S(1)}, u32[]{:S(2)}, u32[]{:S(2)}) collective-permute-start(f32[128,1,32,128]{3,0,2,1:T(8,128)S(1)} %get-tuple-element.19), channel_id=1, source_target_pairs={{0,4},{4,8},{8,12},{12,16},{16,20},{20,24},{24,28},{1,5},{5,9},{9,... | collective-permute-start | bytes 6291464 | tf_op jit(solution)/shard_map/ppermute | solution.py:17
  195.4 47.9 %collective-permute-start.15 = (f32[128,1,32,128]{3,0,2,1:T(8,128)S(1)}, f32[128,1,32,128]{3,0,2,1:T(8,128)S(1)}, u32[]{:S(2)}, u32[]{:S(2)}) collective-permute-start(f32[128,1,32,128]{3,0,2,1:T(8,128)S(1)} %get-tuple-element.20), channel_id=1, source_target_pairs={{4,0},{8,4},{12,8},{16,12},{20,16},{24,20},{28,24},{5,1},{9,5},{13... | collective-permute-start | bytes 6291464 | tf_op jit(solution)/shard_map/ppermute | solution.py:18
  197.8 47.1 %collective-permute-start.16 = (f32[128,4,1,128]{3,0,2,1:T(8,128)S(1)}, f32[128,4,1,128]{3,0,2,1:T(8,128)S(1)}, u32[]{:S(2)}, u32[]{:S(2)}) collective-permute-start(f32[128,4,1,128]{3,0,2,1:T(8,128)S(1)} %get-tuple-element.15), channel_id=1, source_target_pairs={{0,1},{1,2},{2,3},{4,5},{5,6},{6,7},{8,9},{9,10},{10,11},{12,13},{... | collective-permute-start | bytes 786440 | tf_op jit(solution)/shard_map/ppermute | solution.py:17
  201.6 45.8 %collective-permute-start.17 = (f32[128,4,1,128]{3,0,2,1:T(8,128)S(1)}, f32[128,4,1,128]{3,0,2,1:T(8,128)S(1)}, u32[]{:S(2)}, u32[]{:S(2)}) collective-permute-start(f32[128,4,1,128]{3,0,2,1:T(8,128)S(1)} %get-tuple-element.16), channel_id=1, source_target_pairs={{1,0},{2,1},{3,2},{5,4},{6,5},{7,6},{9,8},{10,9},{11,10},{13,12},{... | collective-permute-start | bytes 786440 | tf_op jit(solution)/shard_map/ppermute | solution.py:18
  204.9 38.6 %collective-permute-start.12 = (f32[1,4,32,128]{3,0,2,1:T(1,128)S(1)}, f32[1,4,32,128]{3,0,2,1:T(1,128)S(1)}, u32[]{:S(2)}, u32[]{:S(2)}) collective-permute-start(f32[1,4,32,128]{3,0,2,1:T(1,128)S(1)} %get-tuple-element.17), channel_id=1, source_target_pairs={{0,32},{32,64},{64,96},{1,33},{33,65},{65,97},{2,34},{34,66},{66,9... | collective-permute-start | bytes 196616 | tf_op jit(solution)/shard_map/ppermute | solution.py:17
  238.9 6.0 %collective-permute-start.13 = (f32[1,4,32,128]{3,0,2,1:T(1,128)S(1)}, f32[1,4,32,128]{3,0,2,1:T(1,128)S(1)}, u32[]{:S(2)}, u32[]{:S(2)}) collective-permute-start(f32[1,4,32,128]{3,0,2,1:T(1,128)S(1)} %get-tuple-element.18), channel_id=1, source_target_pairs={{32,0},{64,32},{96,64},{33,1},{65,33},{97,65},{34,2},{66,34},{98,6... | collective-permute-start | bytes 196616 | tf_op jit(solution)/shard_map/ppermute | solution.py:18
  279.4 44.1 %collective-permute-start.20 = (f32[128,1,32,128]{3,0,2,1:T(8,128)S(1)}, f32[128,1,32,128]{3,0,2,1:T(8,128)S(1)}, u32[]{:S(2)}, u32[]{:S(2)}) collective-permute-start(f32[128,1,32,128]{3,0,2,1:T(8,128)S(1)} %get-tuple-element.11), channel_id=1, source_target_pairs={{0,4},{4,8},{8,12},{12,16},{16,20},{20,24},{24,28},{1,5},{5,9},{9,... | collective-permute-start | bytes 6291464 | tf_op jit(solution)/shard_map/ppermute | solution.py:17
  280.9 46.5 %collective-permute-start.21 = (f32[128,1,32,128]{3,0,2,1:T(8,128)S(1)}, f32[128,1,32,128]{3,0,2,1:T(8,128)S(1)}, u32[]{:S(2)}, u32[]{:S(2)}) collective-permute-start(f32[128,1,32,128]{3,0,2,1:T(8,128)S(1)} %get-tuple-element.12), channel_id=1, source_target_pairs={{4,0},{8,4},{12,8},{16,12},{20,16},{24,20},{28,24},{5,1},{9,5},{13... | collective-permute-start | bytes 6291464 | tf_op jit(solution)/shard_map/ppermute | solution.py:18
  283.3 45.7 %collective-permute-start.22 = (f32[128,4,1,128]{3,0,2,1:T(8,128)S(1)}, f32[128,4,1,128]{3,0,2,1:T(8,128)S(1)}, u32[]{:S(2)}, u32[]{:S(2)}) collective-permute-start(f32[128,4,1,128]{3,0,2,1:T(8,128)S(1)} %get-tuple-element.9), channel_id=1, source_target_pairs={{0,1},{1,2},{2,3},{4,5},{5,6},{6,7},{8,9},{9,10},{10,11},{12,13},{... | collective-permute-start | bytes 786440 | tf_op jit(solution)/shard_map/ppermute | solution.py:17
  285.4 45.9 %collective-permute-start.23 = (f32[128,4,1,128]{3,0,2,1:T(8,128)S(1)}, f32[128,4,1,128]{3,0,2,1:T(8,128)S(1)}, u32[]{:S(2)}, u32[]{:S(2)}) collective-permute-start(f32[128,4,1,128]{3,0,2,1:T(8,128)S(1)} %get-tuple-element.10), channel_id=1, source_target_pairs={{1,0},{2,1},{3,2},{5,4},{6,5},{7,6},{9,8},{10,9},{11,10},{13,12},{... | collective-permute-start | bytes 786440 | tf_op jit(solution)/shard_map/ppermute | solution.py:18
  290.4 38.6 %collective-permute-start.18 = (f32[1,4,32,128]{3,0,2,1:T(1,128)S(1)}, f32[1,4,32,128]{3,0,2,1:T(1,128)S(1)}, u32[]{:S(2)}, u32[]{:S(2)}) collective-permute-start(f32[1,4,32,128]{3,0,2,1:T(1,128)S(1)} %get-tuple-element.13), channel_id=1, source_target_pairs={{0,32},{32,64},{64,96},{1,33},{33,65},{65,97},{2,34},{34,66},{66,9... | collective-permute-start | bytes 196616 | tf_op jit(solution)/shard_map/ppermute | solution.py:17
  323.5 5.5 %collective-permute-start.19 = (f32[1,4,32,128]{3,0,2,1:T(1,128)S(1)}, f32[1,4,32,128]{3,0,2,1:T(1,128)S(1)}, u32[]{:S(2)}, u32[]{:S(2)}) collective-permute-start(f32[1,4,32,128]{3,0,2,1:T(1,128)S(1)} %get-tuple-element.14), channel_id=1, source_target_pairs={{32,0},{64,32},{96,64},{33,1},{65,33},{97,65},{34,2},{66,34},{98,6... | collective-permute-start | bytes 196616 | tf_op jit(solution)/shard_map/ppermute | solution.py:18
Sparse Core Ops, SparseCore 0:
  364.4 106.6 all-reduce.18
where the time goes:
time: 504 us; the launch traced here: 497 us
  waiting for transfers between devices  243 us (48%)
  other arithmetic  133 us (26%)
  starting transfers between devices  60.7 us (12%)
  local copies, waits for them, and re-layouts  47 us (9%)
  between operations  14.6 us (3%)
    ppermute x12, waiting for transfers between devices, extended(): lax.ppermute(last, axis, up)  125 us
    psum x1, waiting for transfers between devices, body(): lax.psum((jnp.sum(moved, axis=1, keepdims=True), jnp.sum(moved * moved, a...  95.2 us
    add x3, other arithmetic, conduction_timestep(): return central_point + scaled_conductivity * spread + scaled_heat_supply  88.6 us
    ppermute x12, starting transfers between devices, extended(): lax.ppermute(last, axis, up)  40.9 us
    reduce_sum x1, other arithmetic, body(): jnp.sum(moved, axis=1, keepdims=True)  32.9 us
    unnamed x5, local copies, waits for them, and re-layouts  28.1 us
    ppermute x12, waiting for transfers between devices, extended(): lax.ppermute(initial, axis, [(b, a) for a, b in up])  22.4 us
    ppermute x12, starting transfers between devices, extended(): lax.ppermute(initial, axis, [(b, a) for a, b in up])  19.7 us
  transfers between devices with their start and end apart: 25, of which 17 were waited for; matrix products, arithmetic and copies ran while one was open for 5% of the time, Pallas kernels for 0%

commit v1 on v0

v1 whole, which is shorter than its diff:
```python
import jax
import jax.numpy as jnp
from jax import lax
from jax.experimental import pallas as pl
from jax.experimental.pallas import tpu as pltpu
from jax.sharding import PartitionSpec as P

STEPS = 4
NC = 8
MESH = pl.DeviceIdType.MESH
F32 = jnp.float32


def merge(sum_a, square_a, count_a, sum_b, square_b, count_b):
    gap = sum_a * (1.0 / count_a) - sum_b * (1.0 / count_b)
    weight = count_a * count_b / (count_a + count_b)
    return sum_a + sum_b, square_a + square_b + gap * gap * weight


def main_kernel(
    u_in, k_in, q_in, u_out, f_out,
    field, cond, supply, zsend, zrecv, part, full, ring, across,
    load_sem, out_sem, xs_sem, xr_sem, zs_sem, zr_sem, ys_sem, yr_sem, ss_sem, sr_sem,
):
    rows, cols, height, lanes = u_in.shape
    chunk = rows // NC
    half = chunk // 2
    py, px, pz = lax.axis_index("py"), lax.axis_index("px"), lax.axis_index("pz")
    ny, nx, nz = lax.axis_size("py"), lax.axis_size("px"), lax.axis_size("pz")
    groups = 4
    xq = lax.rem(px, groups)
    zq = px - xq
    right = {"px": zq + lax.rem(xq + 1, groups)}
    left = {"px": zq + lax.rem(xq + groups - 1, groups)}
    partner = {"px": lax.rem(px + groups, nx)}
    x_after, x_before = lax.rem(xq + 1, groups), lax.rem(xq + groups - 1, groups)
    x_far = lax.rem(xq + 2, groups)

    has = {
        ("x", 0): px > 0, ("x", 1): px < nx - 1,
        ("y", 0): py > 0, ("y", 1): py < ny - 1,
        ("z", 0): pz > 0, ("z", 1): pz < nz - 1,
    }
    peer = {
        ("x", 0): {"px": px - 1}, ("x", 1): {"px": px + 1},
        ("y", 0): {"py": py - 1}, ("y", 1): {"py": py + 1},
        ("z", 0): {"pz": pz - 1}, ("z", 1): {"pz": pz + 1},
    }

    barrier = pltpu.get_barrier_semaphore()
    count = jnp.int32(3)
    for key in has:
        count = count + has[key].astype(jnp.int32)

        @pl.when(has[key])
        def _():
            pl.semaphore_signal(barrier, inc=1, device_id=peer[key], device_id_type=MESH)

    for other in (right, left, partner):
        pl.semaphore_signal(barrier, inc=1, device_id=other, device_id_type=MESH)

    def load(c, which):
        span = pl.ds(c * chunk, chunk)
        if which == 0:
            return pltpu.make_async_copy(
                u_in.at[span], field.at[0, pl.ds(c * chunk + 1, chunk), pl.ds(1, cols)], load_sem.at[0, c]
            )
        source, target = ((k_in, cond), (q_in, supply))[which - 1]
        return pltpu.make_async_copy(source.at[span], target.at[span], load_sem.at[which, c])

    def remote(src, dst, send, recv, device):
        return pltpu.make_async_remote_copy(
            src_ref=src, dst_ref=dst, send_sem=send, recv_sem=recv, device_id=device, device_id_type=MESH
        )

    def x_copy(slot, c, side, first=False):
        span = pl.ds(c * chunk, chunk)
        padded = pl.ds(c * chunk + 1, chunk)
        edge = 0 if side == 0 else cols - 1
        src = u_in.at[span, edge] if first else field.at[slot, padded, edge + 1]
        return remote(
            src, field.at[slot, padded, cols + 1 if side == 0 else 0],
            xs_sem.at[side, slot, c], xr_sem.at[1 - side, slot, c], peer["x", side],
        )

    def x_arrival(slot, c, side):
        padded = pl.ds(c * chunk + 1, chunk)
        dst = field.at[slot, padded, 0 if side == 0 else cols + 1]
        return remote(dst, dst, xs_sem.at[side, slot, c], xr_sem.at[side, slot, c], peer["x", side])

    def z_copy(slot, c, side):
        span = pl.ds(c * chunk, chunk)
        return remote(
            zsend.at[slot, side, span], zrecv.at[slot, 1 - side, span],
            zs_sem.at[side, slot, c], zr_sem.at[1 - side, slot, c], peer["z", side],
        )

    def z_arrival(slot, c, side):
        dst = zrecv.at[slot, side, pl.ds(c * chunk, chunk)]
        return remote(dst, dst, zs_sem.at[side, slot, c], zr_sem.at[side, slot, c], peer["z", side])

    def y_copy(slot, side, first=False):
        inner = pl.ds(1, cols)
        row = 0 if side == 0 else rows - 1
        src = u_in.at[row] if first else field.at[slot, row + 1, inner]
        return remote(
            src, field.at[slot, rows + 1 if side == 0 else 0, inner],
            ys_sem.at[side, slot], yr_sem.at[1 - side, slot], peer["y", side],
        )

    def y_arrival(slot, side):
        dst = field.at[slot, 0 if side == 0 else rows + 1, pl.ds(1, cols)]
        return remote(dst, dst, ys_sem.at[side, slot], yr_sem.at[side, slot], peer["y", side])

    for which in range(3):
        @pl.loop(0, NC)
        def _(c):
            load(c, which).start()

    pl.semaphore_wait(barrier, count)

    for side in range(2):
        @pl.when(has["x", side])
        def _():
            @pl.loop(0, NC)
            def _(c):
                x_copy(0, c, side, first=True).start()

        @pl.when(has["y", side])
        def _():
            y_copy(0, side, first=True).start()

    zero_column = jnp.zeros((height, lanes), F32)
    zero_edge = jnp.zeros((cols, lanes), F32)
    for side in range(2):
        @pl.when(jnp.logical_not(has["x", side]))
        def _():
            @pl.loop(0, rows)
            def _(y):
                for slot in range(2):
                    field[slot, y + 1, 0 if side == 0 else cols + 1] = zero_column

        @pl.when(jnp.logical_not(has["y", side]))
        def _():
            for slot in range(2):
                for x in range(cols):
                    field[slot, 0 if side == 0 else rows + 1, x + 1] = zero_column

        @pl.when(jnp.logical_not(has["z", side]))
        def _():
            @pl.loop(0, rows)
            def _(y):
                for slot in range(2):
                    zrecv[slot, side, y] = zero_edge

    def pack(slot, y, x, value):
        zsend[slot, 0, y, x : x + 1] = value[0:1]
        zsend[slot, 1, y, x : x + 1] = value[height - 1 : height]

    @pl.loop(0, NC)
    def _(c):
        load(c, 0).wait()

        @pl.loop(0, chunk)
        def _(r):
            y = c * chunk + r
            for x in range(cols):
                pack(0, y, x, field[0, y + 1, x + 1])

        for side in range(2):
            @pl.when(has["z", side])
            def _():
                z_copy(0, c, side).start()

    row_index = lax.broadcasted_iota(jnp.int32, (height, lanes), 0)
    at_low, at_high = row_index == 0, row_index == height - 1

    def compute(step, c):
        src, dst = step % 2, (step + 1) % 2
        if step == 0:
            load(c, 1).wait()
            load(c, 2).wait()
        for side in range(2):
            @pl.when(has["x", side])
            def _():
                x_arrival(src, c, side).wait_recv()
                if step >= 1:
                    x_copy(dst, c, side).wait_send()

            @pl.when(has["z", side])
            def _():
                z_arrival(src, c, side).wait_recv()
                if step >= 1:
                    z_copy(dst, c, side).wait_send()

            @pl.when(jnp.logical_and(has["y", side], c == (0 if side == 0 else NC - 1)))
            def _():
                y_arrival(src, side).wait_recv()
                if step >= 1:
                    y_copy(dst, side).wait_send()

        @pl.loop(0, chunk)
        def _(r):
            y = c * chunk + r
            fresh = []
            for x in range(cols):
                here = field[src, y + 1, x + 1]
                below = jnp.where(at_low, zrecv[src, 0, y, x : x + 1], pltpu.roll(here, 1, 0))
                above = jnp.where(at_high, zrecv[src, 1, y, x : x + 1], pltpu.roll(here, height - 1, 0))
                spread = (
                    field[src, y, x + 1] + field[src, y + 2, x + 1]
                    + field[src, y + 1, x] + field[src, y + 1, x + 2]
                    + below + above - 6.0 * here
                )
                value = here + cond[y, x] * spread + supply[y, x]
                field[dst, y + 1, x + 1] = value
                if step < STEPS - 1:
                    pack(dst, y, x, value)
                fresh.append(value)
            if step == STEPS - 1:
                total = (fresh[0] + fresh[1]) + (fresh[2] + fresh[3])
                middle = total * (1.0 / cols)
                square = None
                for value in fresh:
                    away = value - middle
                    square = away * away if square is None else square + away * away
                for g in range(groups):
                    part[g, 0, y] = total[8 * g : 8 * g + 8]
                    part[g, 1, y] = square[8 * g : 8 * g + 8]

        if step < STEPS - 1:
            for side in range(2):
                @pl.when(has["x", side])
                def _():
                    x_copy(dst, c, side).start()

                @pl.when(has["z", side])
                def _():
                    z_copy(dst, c, side).start()

                @pl.when(jnp.logical_and(has["y", side], c == (0 if side == 0 else NC - 1)))
                def _():
                    y_copy(dst, side).start()

    for step in range(STEPS - 1):
        @pl.loop(0, NC)
        def _(c):
            compute(step, c)

    last = STEPS % 2

    def u_store(c):
        return pltpu.make_async_copy(
            field.at[last, pl.ds(c * chunk + 1, chunk), pl.ds(1, cols)],
            u_out.at[pl.ds(c * chunk, chunk)], out_sem.at[0, c],
        )

    def f_store(c):
        span = pl.ds(c * chunk, chunk)
        return pltpu.make_async_copy(full.at[:, :, span], f_out.at[:, :, span], out_sem.at[1, c])

    def plus(c):
        return pl.ds(c * chunk, half)

    def minus(c):
        return pl.ds(c * chunk + half, half)

    def whole(c):
        return pl.ds(c * chunk, chunk)

    def stat(kind, c):
        send, recv = ss_sem.at[kind, c], sr_sem.at[kind, c]
        if kind == 0:
            return remote(part.at[x_far, :, plus(c)], ring.at[0, :, c], send, recv, right)
        if kind == 1:
            return remote(part.at[x_far, :, minus(c)], ring.at[1, :, c], send, recv, left)
        if kind == 2:
            return remote(part.at[x_after, :, minus(c)], ring.at[2, :, c], send, recv, right)
        if kind == 3:
            return remote(part.at[x_before, :, plus(c)], ring.at[3, :, c], send, recv, left)
        if kind == 4:
            return remote(part.at[x_after, :, plus(c)], ring.at[4, :, c], send, recv, right)
        if kind == 5:
            return remote(part.at[x_before, :, minus(c)], ring.at[5, :, c], send, recv, left)
        if kind == 6:
            return remote(part.at[xq, :, whole(c)], across.at[:, whole(c)], send, recv, partner)
        if kind == 7:
            return remote(full.at[xq, :, whole(c)], full.at[xq, :, whole(c)], send, recv, right)
        if kind == 8:
            return remote(full.at[xq, :, whole(c)], full.at[xq, :, whole(c)], send, recv, left)
        if kind == 9:
            return remote(full.at[x_before, :, plus(c)], full.at[x_before, :, plus(c)], send, recv, right)
        return remote(full.at[x_after, :, minus(c)], full.at[x_after, :, minus(c)], send, recv, left)

    def stat_arrival(kind, c):
        send, recv = ss_sem.at[kind, c], sr_sem.at[kind, c]
        if kind < 6:
            dst = ring.at[kind, :, c]
        elif kind == 6:
            dst = across.at[:, whole(c)]
        elif kind == 7:
            dst = full.at[x_before, :, whole(c)]
        elif kind == 8:
            dst = full.at[x_after, :, whole(c)]
        elif kind == 9:
            dst = full.at[x_far, :, plus(c)]
        else:
            dst = full.at[x_far, :, minus(c)]
        return remote(dst, dst, send, recv, partner)

    def stage_a(c):
        u_store(c).start()
        for kind in range(4):
            stat(kind, c).start()

    def stage_b(c):
        for kind, owner, offset in ((0, x_after, 0), (1, x_before, half)):
            stat_arrival(kind, c).wait_recv()
            span = pl.ds(c * chunk + offset, half)
            total, square = merge(
                part[owner, 0, span], part[owner, 1, span], 4.0, ring[kind, 0, c], ring[kind, 1, c], 4.0
            )
            part[owner, 0, span] = total
            part[owner, 1, span] = square
            stat(4 + kind, c).start()

    def stage_c(c):
        for kind in (2, 3, 4, 5):
            stat_arrival(kind, c).wait_recv()
        for near, far, offset in ((3, 4, 0), (2, 5, half)):
            span = pl.ds(c * chunk + offset, half)
            total, square = merge(
                part[xq, 0, span], part[xq, 1, span], 4.0, ring[near, 0, c], ring[near, 1, c], 4.0
            )
            total, square = merge(total, square, 8.0, ring[far, 0, c], ring[far, 1, c], 8.0)
            part[xq, 0, span] = total
            part[xq, 1, span] = square
        stat(6, c).start()

    def stage_d(c):
        stat_arrival(6, c).wait_recv()
        for offset in (0, half):
            span = pl.ds(c * chunk + offset, half)
            total, square = merge(part[xq, 0, span], part[xq, 1, span], 16.0, across[0, span], across[1, span], 16.0)
            full[xq, 0, span] = total * (1.0 / 32.0)
            full[xq, 1, span] = lax.rsqrt(square * (1.0 / 32.0) + 0.0001)
        stat(7, c).start()
        stat(8, c).start()

    def stage_e(c):
        stat_arrival(7, c).wait_recv()
        stat(9, c).start()
        stat_arrival(8, c).wait_recv()
        stat(10, c).start()

    def stage_g(c):
        stat_arrival(9, c).wait_recv()
        stat_arrival(10, c).wait_recv()
        f_store(c).start()

    def first_stage(c):
        compute(STEPS - 1, c)
        stage_a(c)

    stages = (first_stage, stage_b, stage_c, stage_d, stage_e, stage_g)

    @pl.loop(0, NC + len(stages) - 1)
    def _(k):
        for delay, stage in enumerate(stages):
            @pl.when(jnp.logical_and(k >= delay, k < NC + delay))
            def _():
                stage(k - delay)

    @pl.loop(0, NC)
    def _(c):
        for side in range(2):
            @pl.when(has["x", side])
            def _():
                x_copy((STEPS - 1) % 2, c, side).wait_send()

            @pl.when(has["z", side])
            def _():
                z_copy((STEPS - 1) % 2, c, side).wait_send()

        for kind in range(11):
            stat(kind, c).wait_send()
        u_store(c).wait()
        f_store(c).wait()

    for side in range(2):
        @pl.when(has["y", side])
        def _():
            y_copy((STEPS - 1) % 2, side).wait_send()


def finish_kernel(u_ref, f_ref, norm_ref, end_ref):
    value = u_ref[...]
    end_ref[...] = value
    for g in range(4):
        band = slice(8 * g, 8 * g + 8)
        norm_ref[:, :, band] = (value[:, :, band] - f_ref[g, 0][:, None]) * f_ref[g, 1][:, None]


def body(u, k, q):
    rows, cols, height, lanes = u.shape
    dma = pltpu.SemaphoreType.DMA
    moved, stats = pl.pallas_call(
        main_kernel,
        out_shape=(
            jax.ShapeDtypeStruct(u.shape, F32),
            jax.ShapeDtypeStruct((4, 2, rows, 8, lanes), F32),
        ),
        in_specs=[pl.BlockSpec(memory_space=pl.ANY)] * 3,
        out_specs=[pl.BlockSpec(memory_space=pl.ANY)] * 2,
        scratch_shapes=[
            pltpu.VMEM((2, rows + 2, cols + 2, height, lanes), F32),
            pltpu.VMEM(u.shape, F32),
            pltpu.VMEM(u.shape, F32),
            pltpu.VMEM((2, 2, rows, cols, lanes), F32),
            pltpu.VMEM((2, 2, rows, cols, lanes), F32),
            pltpu.VMEM((4, 2, rows, 8, lanes), F32),
            pltpu.VMEM((4, 2, rows, 8, lanes), F32),
            pltpu.VMEM((6, 2, NC, rows // NC // 2, 8, lanes), F32),
            pltpu.VMEM((2, rows, 8, lanes), F32),
            dma((3, NC)), dma((2, NC)),
            dma((2, 2, NC)), dma((2, 2, NC)), dma((2, 2, NC)), dma((2, 2, NC)),
            dma((2, 2)), dma((2, 2)), dma((11, NC)), dma((11, NC)),
        ],
        compiler_params=pltpu.CompilerParams(
            collective_id=0, has_side_effects=True, vmem_limit_bytes=62 * 1024 * 1024
        ),
        name="heat_steps",
    )(u, k, q)
    tile = 8
    block = pl.BlockSpec((tile, cols, height, lanes), lambda i: (i, 0, 0, 0))
    return pl.pallas_call(
        finish_kernel,
        grid=(rows // tile,),
        out_shape=(jax.ShapeDtypeStruct(u.shape, F32),) * 2,
        in_specs=[block, pl.BlockSpec((4, 2, tile, 8, lanes), lambda i: (0, 0, i, 0, 0))],
        out_specs=[block, block],
        name="centre_and_scale",
    )(moved, stats)


def solution(mesh):
    placed = P("py", "px", "pz", None)
    return jax.shard_map(
        body, mesh=mesh, in_specs=(placed, placed, placed), out_specs=(placed, placed), check_vma=False
    )
```

time: 504 us -> 395 us (0.78)
  Pallas kernels: 0 us -> 393 us
  waiting for transfers between devices: 243 us -> 0 us
  other arithmetic: 133 us -> 0 us
  starting transfers between devices: 60.7 us -> 0 us
  local copies, waits for them, and re-layouts: 47 us -> 0 us
  between operations: 14.6 us -> 0.64 us
    pallas_call x0 -> x2, Pallas kernels: none -> 393 us  [the longest x1 377 us: body(): pl.pallas_call(main_kernel, out_shape=(jax.ShapeDtypeStruct(u.shape, F32)...]
    ppermute x24 -> x0, waiting for transfers between devices: 147 us -> none  [the longest x12 125 us: extended(): lax.ppermute(last, axis, up)]
    psum x1 -> x0, waiting for transfers between devices: 95.2 us -> none  [body(): lax.psum((jnp.sum(moved, axis=1, keepdims=True), jnp.sum(moved * moved, a...]
    add x3 -> x0, other arithmetic: 88.6 us -> none  [conduction_timestep(): return central_point + scaled_conductivity * spread + scaled_heat_supply]
    ppermute x24 -> x0, starting transfers between devices: 60.6 us -> none  [the longest x12 40.9 us: extended(): lax.ppermute(last, axis, up)]
    reduce_sum x1 -> x0, other arithmetic: 32.9 us -> none  [body(): jnp.sum(moved, axis=1, keepdims=True)]
    unnamed x5 -> x0, local copies, waits for them, and re-layouts: 28.1 us -> none
    slice x12 -> x0, local copies, waits for them, and re-layouts: 16 us -> none  [extended(): last = lax.slice_in_dim(array, length - width, length, axis=dim)]
  transfers between devices with their start and end apart: 25 -> 0, of which waited for: 17 -> 0; matrix products, arithmetic and copies ran while one was open for 5% -> 0% of each run, Pallas kernels for 0% -> 0%
where the time goes in v1:
time: 395 us; the launch traced here: 393 us
  Pallas kernels  393 us (99%)
    pallas_call x1, Pallas kernels, body(): pl.pallas_call(main_kernel, out_shape=(jax.ShapeDtypeStruct(u.shape, F32)...  377 us
    pallas_call x1, Pallas kernels, body(): pl.pallas_call(finish_kernel, grid=(rows // tile,), out_shape=(jax.ShapeD...  15.7 us

profile of v1, /device:TPU:1, one launch (start us, length us, event | category | flops | bytes accessed | tf_op | source)
XLA Modules:
  0.0 393.4 jit_solution(2672261589828444254)
XLA Ops:
  0.6 377.1 %heat_steps.1 = (f32[128,4,32,128]{3,2,1,0:T(8,128)}, f32[4,2,128,8,128]{4,3,2,1,0:T(8,128)}) custom-call(f32[128,4,32,128]{3,2,1,0:T(8,128)} %u_in.1, f32[128,4,32,128]{3,2,1,0:T(8,128)} %k_in.1, f32[128,4,32,128]{3,2,1,0:T(8,128)} %q_in.1), custom_call_target="tpu_custom_call" | custom-call | tf_op jit(solution)/shard_map/heat_steps/pallas_call | solution.py:407
  377.8 15.7 %centre_and_scale.1 = (f32[128,4,32,128]{3,2,1,0:T(8,128)}, f32[128,4,32,128]{3,2,1,0:T(8,128)}) custom-call(f32[128,4,32,128]{3,2,1,0:T(8,128)} %get-tuple-element.4.u_ref, f32[4,2,128,8,128]{4,3,2,1,0:T(8,128)} %get-tuple-element.5.f_ref), custom_call_target="tpu_custom_call" | custom-call | tf_op jit(solution)/shard_map/centre_and_scale/pallas_call | solution.py:436

commit v2 on v1

--- a/solution.py
+++ b/solution.py
@@ -7,6 +7,7 @@
 
 STEPS = 4
 NC = 8
+FIRST = 5
 MESH = pl.DeviceIdType.MESH
 F32 = jnp.float32
 
@@ -19,8 +20,8 @@
 
 def main_kernel(
     u_in, k_in, q_in, u_out, f_out,
-    field, cond, supply, zsend, zrecv, part, full, ring, across,
-    load_sem, out_sem, xs_sem, xr_sem, zs_sem, zr_sem, ys_sem, yr_sem, ss_sem, sr_sem,
+    field, cond, supply, zsend, zrecv, part, full, ring, across, halves, passing,
+    load_sem, out_sem, ps_sem, pr_sem, xs_sem, xr_sem, zs_sem, zr_sem, ys_sem, yr_sem, ss_sem, sr_sem,
 ):
     rows, cols, height, lanes = u_in.shape
     chunk = rows // NC
@@ -83,6 +84,54 @@
             xs_sem.at[side, slot, c], xr_sem.at[1 - side, slot, c], peer["x", side],
         )
 
+    middle = nx // 2
+    at_seam = (px == middle, px == middle - 1)
+    carries = (px == 0, px == nx - 1)
+
+    def odd(c):
+        return lax.rem(c, 2) == 1
+
+    def x_detour(slot, c, side, step):
+        edge = 0 if side == 0 else cols - 1
+        if step == 0:
+            src = u_in.at[pl.ds(c * chunk, chunk), edge]
+        else:
+            src = field.at[slot, pl.ds(c * chunk + 1, chunk), edge + 1]
+        return remote(
+            src, passing.at[step, lax.div(c, 2)],
+            xs_sem.at[side, slot, c], pr_sem.at[step, lax.div(c, 2)], partner,
+        )
+
+    def x_start(step, c, side):
+        slot = step % 2
+        detour = jnp.logical_and(at_seam[side], odd(c))
+
+        @pl.when(detour)
+        def _():
+            x_detour(slot, c, side, step).start()
+
+        @pl.when(jnp.logical_not(detour))
+        def _():
+            x_copy(slot, c, side, step == 0).start()
+
+    def pass_on(step, c, side):
+        here, slot = passing.at[step, lax.div(c, 2)], step % 2
+        return remote(
+            here, field.at[slot, pl.ds(c * chunk + 1, chunk), cols + 1 if side == 0 else 0],
+            ps_sem.at[step, lax.div(c, 2)], xr_sem.at[1 - side, slot, c],
+            {"px": middle - 1 if side == 0 else middle},
+        )
+
+    def relay(step, c):
+        here = passing.at[step, lax.div(c, 2)]
+        for side in range(2):
+            @pl.when(jnp.logical_and(carries[side], odd(c)))
+            def _():
+                remote(
+                    here, here, ps_sem.at[step, lax.div(c, 2)], pr_sem.at[step, lax.div(c, 2)], partner
+                ).wait_recv()
+                pass_on(step, c, side).start()
+
     def x_arrival(slot, c, side):
         padded = pl.ds(c * chunk + 1, chunk)
         dst = field.at[slot, padded, 0 if side == 0 else cols + 1]
@@ -124,7 +173,7 @@
         def _():
             @pl.loop(0, NC)
             def _(c):
-                x_copy(0, c, side, first=True).start()
+                x_start(0, c, side)
 
         @pl.when(has["y", side])
         def _():
@@ -180,6 +229,7 @@
         if step == 0:
             load(c, 1).wait()
             load(c, 2).wait()
+            relay(0, c)
         for side in range(2):
             @pl.when(has["x", side])
             def _():
@@ -232,7 +282,7 @@
             for side in range(2):
                 @pl.when(has["x", side])
                 def _():
-                    x_copy(dst, c, side).start()
+                    x_start(step + 1, c, side)
 
                 @pl.when(has["z", side])
                 def _():
@@ -241,6 +291,15 @@
                 @pl.when(jnp.logical_and(has["y", side], c == (0 if side == 0 else NC - 1)))
                 def _():
                     y_copy(dst, side).start()
+
+            @pl.when(c > 0)
+            def _():
+                relay(step + 1, c - 1)
+
+        if step >= 1:
+            @pl.when(c == 0)
+            def _():
+                relay(step, NC - 1)
 
     for step in range(STEPS - 1):
         @pl.loop(0, NC)
@@ -259,117 +318,176 @@
         span = pl.ds(c * chunk, chunk)
         return pltpu.make_async_copy(full.at[:, :, span], f_out.at[:, :, span], out_sem.at[1, c])
 
-    def plus(c):
-        return pl.ds(c * chunk, half)
-
-    def minus(c):
-        return pl.ds(c * chunk + half, half)
-
-    def whole(c):
-        return pl.ds(c * chunk, chunk)
-
-    def stat(kind, c):
+    lower = lax.div(px, groups)
+
+    def span_of(c, mine):
+        if mine:
+            return c * chunk + lower * half, half // 2
+        return c * chunk, half
+
+    def plus(c, mine):
+        start, size = span_of(c, mine)
+        return pl.ds(start, size)
+
+    def minus(c, mine):
+        start, size = span_of(c, mine)
+        return pl.ds(start + size, size)
+
+    def whole(c, mine):
+        start, size = span_of(c, mine)
+        return pl.ds(start, 2 * size)
+
+    def other(c):
+        return pl.ds(c * chunk + (1 - lower) * half, half)
+
+    def landing(kind, c, mine):
+        return ring.at[kind, :, c, pl.ds(0, half // 2)] if mine else ring.at[kind, :, c]
+
+    def stat(kind, c, mine):
         send, recv = ss_sem.at[kind, c], sr_sem.at[kind, c]
         if kind == 0:
-            return remote(part.at[x_far, :, plus(c)], ring.at[0, :, c], send, recv, right)
+            return remote(part.at[x_far, :, plus(c, mine)], landing(0, c, mine), send, recv, right)
         if kind == 1:
-            return remote(part.at[x_far, :, minus(c)], ring.at[1, :, c], send, recv, left)
+            return remote(part.at[x_far, :, minus(c, mine)], landing(1, c, mine), send, recv, left)
         if kind == 2:
-            return remote(part.at[x_after, :, minus(c)], ring.at[2, :, c], send, recv, right)
+            return remote(part.at[x_after, :, minus(c, mine)], landing(2, c, mine), send, recv, right)
         if kind == 3:
-            return remote(part.at[x_before, :, plus(c)], ring.at[3, :, c], send, recv, left)
+            return remote(part.at[x_before, :, plus(c, mine)], landing(3, c, mine), send, recv, left)
         if kind == 4:
-            return remote(part.at[x_after, :, plus(c)], ring.at[4, :, c], send, recv, right)
+            return remote(part.at[x_after, :, plus(c, mine)], landing(4, c, mine), send, recv, right)
         if kind == 5:
-            return remote(part.at[x_before, :, minus(c)], ring.at[5, :, c], send, recv, left)
+            return remote(part.at[x_before, :, minus(c, mine)], landing(5, c, mine), send, recv, left)
         if kind == 6:
-            return remote(part.at[xq, :, whole(c)], across.at[:, whole(c)], send, recv, partner)
+            if mine:
+                return remote(part.at[:, :, other(c)], halves.at[:, :, pl.ds(c * half, half)], send, recv, partner)
+            return remote(part.at[xq, :, whole(c, mine)], across.at[:, pl.ds((c - FIRST) * chunk, chunk)], send, recv, partner)
         if kind == 7:
-            return remote(full.at[xq, :, whole(c)], full.at[xq, :, whole(c)], send, recv, right)
+            return remote(full.at[xq, :, whole(c, mine)], full.at[xq, :, whole(c, mine)], send, recv, right)
         if kind == 8:
-            return remote(full.at[xq, :, whole(c)], full.at[xq, :, whole(c)], send, recv, left)
+            return remote(full.at[xq, :, whole(c, mine)], full.at[xq, :, whole(c, mine)], send, recv, left)
         if kind == 9:
-            return remote(full.at[x_before, :, plus(c)], full.at[x_before, :, plus(c)], send, recv, right)
-        return remote(full.at[x_after, :, minus(c)], full.at[x_after, :, minus(c)], send, recv, left)
-
-    def stat_arrival(kind, c):
+            return remote(full.at[x_before, :, plus(c, mine)], full.at[x_before, :, plus(c, mine)], send, recv, right)
+        if kind == 10:
+            return remote(full.at[x_after, :, minus(c, mine)], full.at[x_after, :, minus(c, mine)], send, recv, left)
+        return remote(full.at[:, :, whole(c, mine)], full.at[:, :, whole(c, mine)], send, recv, partner)
+
+    def stat_arrival(kind, c, mine):
         send, recv = ss_sem.at[kind, c], sr_sem.at[kind, c]
         if kind < 6:
-            dst = ring.at[kind, :, c]
+            dst = landing(kind, c, mine)
         elif kind == 6:
-            dst = across.at[:, whole(c)]
+            dst = halves.at[:, :, pl.ds(c * half, half)] if mine else across.at[:, pl.ds((c - FIRST) * chunk, chunk)]
         elif kind == 7:
-            dst = full.at[x_before, :, whole(c)]
+            dst = full.at[x_before, :, whole(c, mine)]
         elif kind == 8:
-            dst = full.at[x_after, :, whole(c)]
+            dst = full.at[x_after, :, whole(c, mine)]
         elif kind == 9:
-            dst = full.at[x_far, :, plus(c)]
+            dst = full.at[x_far, :, plus(c, mine)]
+        elif kind == 10:
+            dst = full.at[x_far, :, minus(c, mine)]
         else:
-            dst = full.at[x_far, :, minus(c)]
+            dst = full.at[:, :, other(c)]
         return remote(dst, dst, send, recv, partner)
 
-    def stage_a(c):
+    def begin(c, mine):
         u_store(c).start()
+        if mine:
+            stat(6, c, mine).start()
+        else:
+            for kind in range(4):
+                stat(kind, c, mine).start()
+
+    def join_halves(c, mine):
+        stat_arrival(6, c, mine).wait_recv()
+        span, there = whole(c, mine), pl.ds(c * half, half)
+        for g in range(groups):
+            total, square = merge(part[g, 0, span], part[g, 1, span], 4.0, halves[g, 0, there], halves[g, 1, there], 4.0)
+            part[g, 0, span] = total
+            part[g, 1, span] = square
         for kind in range(4):
-            stat(kind, c).start()
-
-    def stage_b(c):
-        for kind, owner, offset in ((0, x_after, 0), (1, x_before, half)):
-            stat_arrival(kind, c).wait_recv()
-            span = pl.ds(c * chunk + offset, half)
-            total, square = merge(
-                part[owner, 0, span], part[owner, 1, span], 4.0, ring[kind, 0, c], ring[kind, 1, c], 4.0
-            )
+            stat(kind, c, mine).start()
+
+    def arrived(kind, c, mine):
+        if mine:
+            return ring[kind, 0, c, pl.ds(0, half // 2)], ring[kind, 1, c, pl.ds(0, half // 2)]
+        return ring[kind, 0, c], ring[kind, 1, c]
+
+    def hand_on_sums(c, mine):
+        one = 8.0 if mine else 4.0
+        for kind, owner, span in ((0, x_after, plus(c, mine)), (1, x_before, minus(c, mine))):
+            stat_arrival(kind, c, mine).wait_recv()
+            total, square = merge(part[owner, 0, span], part[owner, 1, span], one, *arrived(kind, c, mine), one)
             part[owner, 0, span] = total
             part[owner, 1, span] = square
-            stat(4 + kind, c).start()
-
-    def stage_c(c):
+            stat(4 + kind, c, mine).start()
+
+    def finish(total, square, span):
+        full[xq, 0, span] = total * (1.0 / 32.0)
+        full[xq, 1, span] = lax.rsqrt(square * (1.0 / 32.0) + 0.0001)
+
+    def own_sums(c, mine):
+        one = 8.0 if mine else 4.0
         for kind in (2, 3, 4, 5):
-            stat_arrival(kind, c).wait_recv()
-        for near, far, offset in ((3, 4, 0), (2, 5, half)):
-            span = pl.ds(c * chunk + offset, half)
-            total, square = merge(
-                part[xq, 0, span], part[xq, 1, span], 4.0, ring[near, 0, c], ring[near, 1, c], 4.0
-            )
-            total, square = merge(total, square, 8.0, ring[far, 0, c], ring[far, 1, c], 8.0)
-            part[xq, 0, span] = total
-            part[xq, 1, span] = square
-        stat(6, c).start()
-
-    def stage_d(c):
-        stat_arrival(6, c).wait_recv()
+            stat_arrival(kind, c, mine).wait_recv()
+        for near, far, span in ((3, 4, plus(c, mine)), (2, 5, minus(c, mine))):
+            total, square = merge(part[xq, 0, span], part[xq, 1, span], one, *arrived(near, c, mine), one)
+            total, square = merge(total, square, 2 * one, *arrived(far, c, mine), 2 * one)
+            if mine:
+                finish(total, square, span)
+            else:
+                part[xq, 0, span] = total
+                part[xq, 1, span] = square
+        if mine:
+            stat(7, c, mine).start()
+            stat(8, c, mine).start()
+        else:
+            stat(6, c, mine).start()
+
+    def join_partner(c, mine):
+        stat_arrival(6, c, mine).wait_recv()
         for offset in (0, half):
-            span = pl.ds(c * chunk + offset, half)
-            total, square = merge(part[xq, 0, span], part[xq, 1, span], 16.0, across[0, span], across[1, span], 16.0)
-            full[xq, 0, span] = total * (1.0 / 32.0)
-            full[xq, 1, span] = lax.rsqrt(square * (1.0 / 32.0) + 0.0001)
-        stat(7, c).start()
-        stat(8, c).start()
-
-    def stage_e(c):
-        stat_arrival(7, c).wait_recv()
-        stat(9, c).start()
-        stat_arrival(8, c).wait_recv()
-        stat(10, c).start()
-
-    def stage_g(c):
-        stat_arrival(9, c).wait_recv()
-        stat_arrival(10, c).wait_recv()
+            span, there = pl.ds(c * chunk + offset, half), pl.ds((c - FIRST) * chunk + offset, half)
+            finish(*merge(part[xq, 0, span], part[xq, 1, span], 16.0, across[0, there], across[1, there], 16.0), span)
+        stat(7, c, mine).start()
+        stat(8, c, mine).start()
+
+    def hand_on_results(c, mine):
+        stat_arrival(7, c, mine).wait_recv()
+        stat(9, c, mine).start()
+        stat_arrival(8, c, mine).wait_recv()
+        stat(10, c, mine).start()
+
+    def collect(c, mine):
+        stat_arrival(9, c, mine).wait_recv()
+        stat_arrival(10, c, mine).wait_recv()
+        if mine:
+            stat(11, c, mine).start()
+        else:
+            f_store(c).start()
+
+    def last_half(c, mine):
+        stat_arrival(11, c, mine).wait_recv()
         f_store(c).start()
 
-    def first_stage(c):
-        compute(STEPS - 1, c)
-        stage_a(c)
-
-    stages = (first_stage, stage_b, stage_c, stage_d, stage_e, stage_g)
-
-    @pl.loop(0, NC + len(stages) - 1)
+    rounds = {
+        True: (begin, join_halves, hand_on_sums, own_sums, hand_on_results, collect, last_half),
+        False: (begin, hand_on_sums, own_sums, join_partner, hand_on_results, collect),
+    }
+    bounds = {True: (0, FIRST), False: (FIRST, NC)}
+
+    @pl.loop(0, NC + 6)
     def _(k):
-        for delay, stage in enumerate(stages):
-            @pl.when(jnp.logical_and(k >= delay, k < NC + delay))
-            def _():
-                stage(k - delay)
+        @pl.when(k < NC)
+        def _():
+            compute(STEPS - 1, k)
+
+        for delay in range(7):
+            for mine in (True, False):
+                low, high = bounds[mine]
+                if delay < len(rounds[mine]) and low < high:
+                    @pl.when(jnp.logical_and(k >= low + delay, k < high + delay))
+                    def _():
+                        rounds[mine][delay](k - delay, mine)
 
     @pl.loop(0, NC)
     def _(c):
@@ -382,8 +500,20 @@
             def _():
                 z_copy((STEPS - 1) % 2, c, side).wait_send()
 
-        for kind in range(11):
-            stat(kind, c).wait_send()
+        for side in range(2):
+            @pl.when(jnp.logical_and(carries[side], odd(c)))
+            def _():
+                for step in range(STEPS):
+                    pass_on(step, c, side).wait_send()
+
+        for mine in (True, False):
+            low, high = bounds[mine]
+
+            @pl.when(jnp.logical_and(c >= low, c < high))
+            def _():
+                for kind in range(12 if mine else 11):
+                    stat(kind, c, mine).wait_send()
+
         u_store(c).wait()
         f_store(c).wait()
 
@@ -421,17 +551,19 @@
             pltpu.VMEM((4, 2, rows, 8, lanes), F32),
             pltpu.VMEM((4, 2, rows, 8, lanes), F32),
             pltpu.VMEM((6, 2, NC, rows // NC // 2, 8, lanes), F32),
-            pltpu.VMEM((2, rows, 8, lanes), F32),
-            dma((3, NC)), dma((2, NC)),
+            pltpu.VMEM((2, max(NC - FIRST, 1) * (rows // NC), 8, lanes), F32),
+            pltpu.VMEM((4, 2, max(FIRST, 1) * (rows // NC // 2), 8, lanes), F32),
+            pltpu.VMEM((STEPS, NC // 2, rows // NC, height, lanes), F32),
+            dma((3, NC)), dma((2, NC)), dma((STEPS, NC // 2)), dma((STEPS, NC // 2)),
             dma((2, 2, NC)), dma((2, 2, NC)), dma((2, 2, NC)), dma((2, 2, NC)),
-            dma((2, 2)), dma((2, 2)), dma((11, NC)), dma((11, NC)),
+            dma((2, 2)), dma((2, 2)), dma((12, NC)), dma((12, NC)),
         ],
         compiler_params=pltpu.CompilerParams(
-            collective_id=0, has_side_effects=True, vmem_limit_bytes=62 * 1024 * 1024
+            collective_id=0, has_side_effects=True, vmem_limit_bytes=63 * 1024 * 1024
         ),
         name="heat_steps",
     )(u, k, q)
-    tile = 8
+    tile = 32
     block = pl.BlockSpec((tile, cols, height, lanes), lambda i: (i, 0, 0, 0))
     return pl.pallas_call(
         finish_kernel,

time: 395 us -> 260 us (0.66)
  Pallas kernels: 393 us -> 259 us
    pallas_call x1, Pallas kernels: 377 us -> 249 us  [body(): pl.pallas_call(main_kernel, out_shape=(jax.ShapeDtypeStruct(u.shape, F32)...]
    pallas_call x1, Pallas kernels: 15.7 us -> 10.3 us  [body(): pl.pallas_call(finish_kernel, grid=(rows // tile,), out_shape=(jax.ShapeD...]
where the time goes in v2:
time: 260 us
  Pallas kernels  259 us (100%)
    pallas_call x1, Pallas kernels, body(): pl.pallas_call(main_kernel, out_shape=(jax.ShapeDtypeStruct(u.shape, F32)...  249 us
    pallas_call x1, Pallas kernels, body(): pl.pallas_call(finish_kernel, grid=(rows // tile,), out_shape=(jax.ShapeD...  10.3 us

profile of v2, /device:TPU:1, one launch (start us, length us, event | category | flops | bytes accessed | tf_op | source)
XLA Modules:
  0.0 259.6 jit_solution(3100706961333595708)
XLA Ops:
  0.6 248.7 %heat_steps.1 = (f32[128,4,32,128]{3,2,1,0:T(8,128)}, f32[4,2,128,8,128]{4,3,2,1,0:T(8,128)}) custom-call(f32[128,4,32,128]{3,2,1,0:T(8,128)} %u_in.1, f32[128,4,32,128]{3,2,1,0:T(8,128)} %k_in.1, f32[128,4,32,128]{3,2,1,0:T(8,128)} %q_in.1), custom_call_target="tpu_custom_call" | custom-call | tf_op jit(solution)/shard_map/heat_steps/pallas_call | solution.py:537
  249.3 10.3 %centre_and_scale.1 = (f32[128,4,32,128]{3,2,1,0:T(8,128)}, f32[128,4,32,128]{3,2,1,0:T(8,128)}) custom-call(f32[128,4,32,128]{3,2,1,0:T(8,128)} %get-tuple-element.4.u_ref, f32[4,2,128,8,128]{4,3,2,1,0:T(8,128)} %get-tuple-element.5.f_ref), custom_call_target="tpu_custom_call" | custom-call | tf_op jit(solution)/shard_map/centre_and_scale/pallas_call | solution.py:568

commit v3 on v2

--- a/solution.py
+++ b/solution.py
@@ -7,6 +7,7 @@
 
 STEPS = 4
 NC = 8
+LEAD = 3
 FIRST = 5
 MESH = pl.DeviceIdType.MESH
 F32 = jnp.float32
@@ -19,9 +20,9 @@
 
 
 def main_kernel(
-    u_in, k_in, q_in, u_out, f_out,
-    field, cond, supply, zsend, zrecv, part, full, ring, across, halves, passing,
-    load_sem, out_sem, ps_sem, pr_sem, xs_sem, xr_sem, zs_sem, zr_sem, ys_sem, yr_sem, ss_sem, sr_sem,
+    u_in, k_in, q_in, cond, full,
+    field, supply, zsend, zrecv, part, ring, across, halves, passing,
+    load_sem, ps_sem, pr_sem, xs_sem, xr_sem, zs_sem, zr_sem, ys_sem, yr_sem, ss_sem, sr_sem,
 ):
     rows, cols, height, lanes = u_in.shape
     chunk = rows // NC
@@ -171,7 +172,7 @@
     for side in range(2):
         @pl.when(has["x", side])
         def _():
-            @pl.loop(0, NC)
+            @pl.loop(0, LEAD)
             def _(c):
                 x_start(0, c, side)
 
@@ -224,12 +225,22 @@
     row_index = lax.broadcasted_iota(jnp.int32, (height, lanes), 0)
     at_low, at_high = row_index == 0, row_index == height - 1
 
+    def send_faces(step, c):
+        for side in range(2):
+            @pl.when(has["x", side])
+            def _():
+                x_start(step, c, side)
+
     def compute(step, c):
         src, dst = step % 2, (step + 1) % 2
         if step == 0:
             load(c, 1).wait()
             load(c, 2).wait()
-            relay(0, c)
+
+            @pl.when(c < LEAD - 1)
+            def _():
+                relay(0, c)
+
         for side in range(2):
             @pl.when(has["x", side])
             def _():
@@ -263,9 +274,11 @@
                     + below + above - 6.0 * here
                 )
                 value = here + cond[y, x] * spread + supply[y, x]
-                field[dst, y + 1, x + 1] = value
                 if step < STEPS - 1:
+                    field[dst, y + 1, x + 1] = value
                     pack(dst, y, x, value)
+                else:
+                    cond[y, x] = value
                 fresh.append(value)
             if step == STEPS - 1:
                 total = (fresh[0] + fresh[1]) + (fresh[2] + fresh[3])
@@ -280,10 +293,6 @@
 
         if step < STEPS - 1:
             for side in range(2):
-                @pl.when(has["x", side])
-                def _():
-                    x_start(step + 1, c, side)
-
                 @pl.when(has["z", side])
                 def _():
                     z_copy(dst, c, side).start()
@@ -292,31 +301,20 @@
                 def _():
                     y_copy(dst, side).start()
 
-            @pl.when(c > 0)
-            def _():
-                relay(step + 1, c - 1)
-
-        if step >= 1:
-            @pl.when(c == 0)
-            def _():
-                relay(step, NC - 1)
+        for ahead, act in ((LEAD, send_faces), (LEAD - 1, relay)):
+            @pl.when(c < NC - ahead)
+            def _():
+                act(step, c + ahead)
+
+            if step < STEPS - 1:
+                @pl.when(c >= NC - ahead)
+                def _():
+                    act(step + 1, c + ahead - NC)
 
     for step in range(STEPS - 1):
         @pl.loop(0, NC)
         def _(c):
             compute(step, c)
-
-    last = STEPS % 2
-
-    def u_store(c):
-        return pltpu.make_async_copy(
-            field.at[last, pl.ds(c * chunk + 1, chunk), pl.ds(1, cols)],
-            u_out.at[pl.ds(c * chunk, chunk)], out_sem.at[0, c],
-        )
-
-    def f_store(c):
-        span = pl.ds(c * chunk, chunk)
-        return pltpu.make_async_copy(full.at[:, :, span], f_out.at[:, :, span], out_sem.at[1, c])
 
     lower = lax.div(px, groups)
 
@@ -390,7 +388,6 @@
         return remote(dst, dst, send, recv, partner)
 
     def begin(c, mine):
-        u_store(c).start()
         if mine:
             stat(6, c, mine).start()
         else:
@@ -462,12 +459,9 @@
         stat_arrival(10, c, mine).wait_recv()
         if mine:
             stat(11, c, mine).start()
-        else:
-            f_store(c).start()
 
     def last_half(c, mine):
         stat_arrival(11, c, mine).wait_recv()
-        f_store(c).start()
 
     rounds = {
         True: (begin, join_halves, hand_on_sums, own_sums, hand_on_results, collect, last_half),
@@ -514,8 +508,6 @@
                 for kind in range(12 if mine else 11):
                     stat(kind, c, mine).wait_send()
 
-        u_store(c).wait()
-        f_store(c).wait()
 
     for side in range(2):
         @pl.when(has["y", side])
@@ -523,12 +515,27 @@
             y_copy((STEPS - 1) % 2, side).wait_send()
 
 
-def finish_kernel(u_ref, f_ref, norm_ref, end_ref):
-    value = u_ref[...]
-    end_ref[...] = value
-    for g in range(4):
-        band = slice(8 * g, 8 * g + 8)
-        norm_ref[:, :, band] = (value[:, :, band] - f_ref[g, 0][:, None]) * f_ref[g, 1][:, None]
+def finish_kernel(u_ref, f_ref, norm_ref, end_ref, sem):
+    step = pl.program_id(0)
+    out = pltpu.make_async_copy(u_ref, end_ref, sem)
+
+    @pl.when(step == 0)
+    def _():
+        out.start()
+
+    tile = norm_ref.shape[0]
+
+    @pl.loop(0, tile)
+    def _(r):
+        y = step * tile + r
+        for x in range(u_ref.shape[1]):
+            for g in range(4):
+                band = slice(8 * g, 8 * g + 8)
+                norm_ref[r, x, band] = (u_ref[y, x, band] - f_ref[g, 0, y]) * f_ref[g, 1, y]
+
+    @pl.when(step == pl.num_programs(0) - 1)
+    def _():
+        out.wait()
 
 
 def body(u, k, q):
@@ -537,40 +544,42 @@
     moved, stats = pl.pallas_call(
         main_kernel,
         out_shape=(
-            jax.ShapeDtypeStruct(u.shape, F32),
-            jax.ShapeDtypeStruct((4, 2, rows, 8, lanes), F32),
+            pltpu.VMEM(u.shape, F32),
+            pltpu.VMEM((4, 2, rows, 8, lanes), F32),
         ),
         in_specs=[pl.BlockSpec(memory_space=pl.ANY)] * 3,
-        out_specs=[pl.BlockSpec(memory_space=pl.ANY)] * 2,
+        out_specs=[pl.BlockSpec(memory_space=pltpu.VMEM)] * 2,
         scratch_shapes=[
             pltpu.VMEM((2, rows + 2, cols + 2, height, lanes), F32),
             pltpu.VMEM(u.shape, F32),
-            pltpu.VMEM(u.shape, F32),
             pltpu.VMEM((2, 2, rows, cols, lanes), F32),
             pltpu.VMEM((2, 2, rows, cols, lanes), F32),
-            pltpu.VMEM((4, 2, rows, 8, lanes), F32),
             pltpu.VMEM((4, 2, rows, 8, lanes), F32),
             pltpu.VMEM((6, 2, NC, rows // NC // 2, 8, lanes), F32),
             pltpu.VMEM((2, max(NC - FIRST, 1) * (rows // NC), 8, lanes), F32),
             pltpu.VMEM((4, 2, max(FIRST, 1) * (rows // NC // 2), 8, lanes), F32),
             pltpu.VMEM((STEPS, NC // 2, rows // NC, height, lanes), F32),
-            dma((3, NC)), dma((2, NC)), dma((STEPS, NC // 2)), dma((STEPS, NC // 2)),
+            dma((3, NC)), dma((STEPS, NC // 2)), dma((STEPS, NC // 2)),
             dma((2, 2, NC)), dma((2, 2, NC)), dma((2, 2, NC)), dma((2, 2, NC)),
             dma((2, 2)), dma((2, 2)), dma((12, NC)), dma((12, NC)),
         ],
         compiler_params=pltpu.CompilerParams(
-            collective_id=0, has_side_effects=True, vmem_limit_bytes=63 * 1024 * 1024
+            collective_id=0, has_side_effects=True, vmem_limit_bytes=49 * 1024 * 1024
         ),
         name="heat_steps",
     )(u, k, q)
-    tile = 32
-    block = pl.BlockSpec((tile, cols, height, lanes), lambda i: (i, 0, 0, 0))
+    tile = 16
     return pl.pallas_call(
         finish_kernel,
         grid=(rows // tile,),
         out_shape=(jax.ShapeDtypeStruct(u.shape, F32),) * 2,
-        in_specs=[block, pl.BlockSpec((4, 2, tile, 8, lanes), lambda i: (0, 0, i, 0, 0))],
-        out_specs=[block, block],
+        in_specs=[pl.BlockSpec(memory_space=pltpu.VMEM)] * 2,
+        out_specs=[
+            pl.BlockSpec((tile, cols, height, lanes), lambda i: (i, 0, 0, 0)),
+            pl.BlockSpec(memory_space=pl.ANY),
+        ],
+        scratch_shapes=[dma],
+        compiler_params=pltpu.CompilerParams(vmem_limit_bytes=8 * 1024 * 1024),
         name="centre_and_scale",
     )(moved, stats)
 

time: 260 us -> 253 us (0.973)
  Pallas kernels: 259 us -> 253 us
    pallas_call x1, Pallas kernels: 249 us -> 245 us  [body(): pl.pallas_call(main_kernel, out_shape=(pltpu.VMEM(u.shape, F32), pltpu.VM...]
    pallas_call x1, Pallas kernels: 10.3 us -> 7.5 us  [body(): pl.pallas_call(finish_kernel, grid=(rows // tile,), out_shape=(jax.ShapeD...]
where the time goes in v3:
time: 253 us
  Pallas kernels  253 us (100%)
    pallas_call x1, Pallas kernels, body(): pl.pallas_call(main_kernel, out_shape=(pltpu.VMEM(u.shape, F32), pltpu.VM...  245 us
    pallas_call x1, Pallas kernels, body(): pl.pallas_call(finish_kernel, grid=(rows // tile,), out_shape=(jax.ShapeD...  7.5 us

profile of v3, /device:TPU:1, one launch (start us, length us, event | category | flops | bytes accessed | tf_op | source)
XLA Modules:
  0.0 253.2 jit_solution(825701641439718238)
XLA Ops:
  0.6 245.1 %heat_steps.1 = (f32[128,4,32,128]{3,2,1,0:T(8,128)S(1)}, f32[4,2,128,8,128]{4,3,2,1,0:T(8,128)S(1)}) custom-call(f32[128,4,32,128]{3,2,1,0:T(8,128)} %u_in.1, f32[128,4,32,128]{3,2,1,0:T(8,128)} %k_in.1, f32[128,4,32,128]{3,2,1,0:T(8,128)} %q_in.1), custom_call_target="tpu_custom_call" | custom-call | tf_op jit(solution)/shard_map/heat_steps/pallas_call | solution.py:544
  245.7 7.5 %centre_and_scale.1 = (f32[128,4,32,128]{3,2,1,0:T(8,128)}, f32[128,4,32,128]{3,2,1,0:T(8,128)}) custom-call(f32[128,4,32,128]{3,2,1,0:T(8,128)S(1)} %get-tuple-element.4.u_ref, f32[4,2,128,8,128]{4,3,2,1,0:T(8,128)S(1)} %get-tuple-element.5.f_ref), custom_call_target="tpu_custom_call" | custom-call | tf_op jit(solution)/shard_map/centre_and_scale/pallas_call | solution.py:572

commit v4 on v3

--- a/solution.py
+++ b/solution.py
@@ -8,7 +8,7 @@
 STEPS = 4
 NC = 8
 LEAD = 3
-FIRST = 5
+FIRST = 6
 MESH = pl.DeviceIdType.MESH
 F32 = jnp.float32
 
@@ -517,13 +517,13 @@
 
 def finish_kernel(u_ref, f_ref, norm_ref, end_ref, sem):
     step = pl.program_id(0)
-    out = pltpu.make_async_copy(u_ref, end_ref, sem)
-
-    @pl.when(step == 0)
-    def _():
-        out.start()
-
     tile = norm_ref.shape[0]
+
+    def out(piece):
+        span = pl.ds(piece * tile, tile)
+        return pltpu.make_async_copy(u_ref.at[span], end_ref.at[span], sem.at[piece])
+
+    out(step).start()
 
     @pl.loop(0, tile)
     def _(r):
@@ -535,7 +535,9 @@
 
     @pl.when(step == pl.num_programs(0) - 1)
     def _():
-        out.wait()
+        @pl.loop(0, pl.num_programs(0))
+        def _(piece):
+            out(piece).wait()
 
 
 def body(u, k, q):
@@ -568,7 +570,7 @@
         ),
         name="heat_steps",
     )(u, k, q)
-    tile = 16
+    tile = 32
     return pl.pallas_call(
         finish_kernel,
         grid=(rows // tile,),
@@ -578,7 +580,7 @@
             pl.BlockSpec((tile, cols, height, lanes), lambda i: (i, 0, 0, 0)),
             pl.BlockSpec(memory_space=pl.ANY),
         ],
-        scratch_shapes=[dma],
+        scratch_shapes=[dma((rows // tile,))],
         compiler_params=pltpu.CompilerParams(vmem_limit_bytes=8 * 1024 * 1024),
         name="centre_and_scale",
     )(moved, stats)

time: 253 us -> 251 us (level)
  Pallas kernels: 253 us -> 250 us
where the time goes in v4:
time: 251 us
  Pallas kernels  250 us (100%)
    pallas_call x1, Pallas kernels, body(): pl.pallas_call(main_kernel, out_shape=(pltpu.VMEM(u.shape, F32), pltpu.VM...  243 us
    pallas_call x1, Pallas kernels, body(): pl.pallas_call(finish_kernel, grid=(rows // tile,), out_shape=(jax.ShapeD...  6.6 us

profile of v4, /device:TPU:1, one launch (start us, length us, event | category | flops | bytes accessed | tf_op | source)
XLA Modules:
  0.0 250.6 jit_solution(7348470933727442909)
XLA Ops:
  0.6 243.3 %heat_steps.1 = (f32[128,4,32,128]{3,2,1,0:T(8,128)S(1)}, f32[4,2,128,8,128]{4,3,2,1,0:T(8,128)S(1)}) custom-call(f32[128,4,32,128]{3,2,1,0:T(8,128)} %u_in.1, f32[128,4,32,128]{3,2,1,0:T(8,128)} %k_in.1, f32[128,4,32,128]{3,2,1,0:T(8,128)} %q_in.1), custom_call_target="tpu_custom_call" | custom-call | tf_op jit(solution)/shard_map/heat_steps/pallas_call | solution.py:546
  244.0 6.6 %centre_and_scale.1 = (f32[128,4,32,128]{3,2,1,0:T(8,128)}, f32[128,4,32,128]{3,2,1,0:T(8,128)}) custom-call(f32[128,4,32,128]{3,2,1,0:T(8,128)S(1)} %get-tuple-element.4.u_ref, f32[4,2,128,8,128]{4,3,2,1,0:T(8,128)S(1)} %get-tuple-element.5.f_ref), custom_call_target="tpu_custom_call" | custom-call | tf_op jit(solution)/shard_map/centre_and_scale/pallas_call | solution.py:574
